TPU v7x, 32 devices: a whole 2x2x4 slice. The times are simulated.
32 devices in a mesh: parts: 2 (over x), inner: 16 (over z, y, core).
Axes of the slice: x: 2, y: 2, z: 4, core: 2. Of those that a mesh axis runs over, the one named last changes fastest.
Arguments:
- stem_slab: bfloat16 [2, 16384, 1024], P(None, ('parts', 'inner')), parts along dimension 1, may hold values from -6 to 6
- branches: bfloat16 [3, 2, 1024, 1024], P(None, None, 'inner'), may hold values from -0.1875 to 0.1875
- column_order: int32 [3, 1024], replicated, may hold values from 0 to 1023, each once within a row
Outputs:
- result_slab: bfloat16 [2, 16384, 1024], P(None, ('parts', 'inner')), parts along dimension 1
There are 2 independent parts, one for each index of `parts`. A program takes and returns all parts, laid end to end along the dimension named above; an argument that names none is the same for every part. Nothing has to cross between parts.
Inputs may be any that keep to these rules, and one draw needn't show every extreme that they name: Each row of column_order names every number from 0 to 1023 exactly once.
All inputs are finite; a program needn't handle non-finite values.
Results may differ from a plain program's by a relative error of at most 0.0057.
Values may be sent and summed in bfloat16 or wider, within the bound.
A program may use at most 64 MiB of HBM per device.

v0:
```python
import functools

import jax
import jax.numpy as jnp
from jax import lax
from jax.experimental import pallas as pl
from jax.experimental.pallas import tpu as pltpu
from jax.sharding import PartitionSpec as P

CORES = 2
YS = 2
CHUNKS = 4
TILE = 256
LANES = 128
F32 = jnp.float32
BF16 = jnp.bfloat16
MESH_ID = pl.DeviceIdType.MESH


def add_block(ordered, block_rows):
    real_part = jnp.dot(ordered[0], block_rows[0], preferred_element_type=F32) - jnp.dot(
        ordered[1], block_rows[1], preferred_element_type=F32
    )
    imag_part = jnp.dot(ordered[0], block_rows[1], preferred_element_type=F32) + jnp.dot(
        ordered[1], block_rows[0], preferred_element_type=F32
    )
    return jnp.stack([real_part, imag_part])


def folded(slab, order_row, branch_slice):
    ordered = jnp.take(slab, order_row, axis=2)
    summed = add_block(ordered, lax.all_gather(branch_slice, "inner", axis=1, tiled=True))
    return summed.astype(BF16)


def plain(stem_slab, branches, column_order):
    current = folded(stem_slab, column_order[0], branches[0])
    for section_index in range(1, branches.shape[0]):
        current = lax.all_to_all(current, "inner", split_axis=2, concat_axis=2, tiled=True)
        current = folded(current, column_order[section_index], branches[section_index])
    return current


def kernel(
    n, stem_hbm, branches, order, out_hbm, stem, out, gathered, onehot, picked, wide, send, recv,
    own_sem, zs_sem, zr_sem, xs_sem, xr_sem, ys_sem, yr_sem, ds_sem, dr_sem, cs_sem, cr_sem, as_sem, ar_sem,
    in_sem, out_sem,
):
    sections = branches.shape[0]
    depth = branches.shape[2]
    total = n * depth
    columns = branches.shape[3]
    chunk = send.shape[3]
    plane = CORES * YS
    nz = n // plane
    me = lax.axis_index("inner")
    x = lax.axis_index("parts")
    z = me // plane
    low = me % plane
    y = low // CORES
    core = low % CORES
    other_low = (1 - y) * CORES + core
    x_peer = {"parts": 1 - x}
    y_peer = {"inner": z * plane + other_low}
    core_peer = {"inner": z * plane + y * CORES + (1 - core)}

    stem_copy = pltpu.make_async_copy(stem_hbm, stem, in_sem)
    stem_copy.start()

    barrier = pltpu.get_barrier_semaphore()

    @pl.loop(1, n)
    def _(hop):
        pl.semaphore_signal(
            barrier, inc=1, device_id={"inner": lax.rem(me + hop, n)}, device_id_type=MESH_ID
        )

    pl.semaphore_signal(barrier, inc=1, device_id=x_peer, device_id_type=MESH_ID)
    pl.semaphore_wait(barrier, n)

    def remote(src, dst, send_sem, recv_sem, device):
        return pltpu.make_async_remote_copy(
            src_ref=src, dst_ref=dst, send_sem=send_sem, recv_sem=recv_sem,
            device_id=device, device_id_type=MESH_ID,
        )

    def block(s, zz, across, p, own=False):
        slot = zz * plane + (other_low if across else low)
        return (branches.at[s, p] if own else gathered.at[s, slot, p]), gathered.at[s, slot, p]

    def z_of(t, way):
        return z - t if way == 0 else z + t

    def z_copy(s, t, way):
        src, dst = block(s, z_of(t, way), False, x, own=t == 0)
        target = {"inner": me + plane if way == 0 else me - plane}
        return remote(src, dst, zs_sem.at[s, t, way], zr_sem.at[s, t, way], target)

    def z_sends(t, way):
        return (z - t >= 0) & (z + 1 < nz) if way == 0 else (z + t < nz) & (z >= 1)

    def z_holds(t, way):
        return z - t >= 0 if way == 0 else z + t < nz

    def x_copy(s, zz):
        src, dst = block(s, zz, False, x)
        return remote(src, dst, xs_sem.at[s, zz], xr_sem.at[s, zz], x_peer)

    def y_copy(s, zz, own=False):
        src, dst = block(s, zz, False, x, own)
        return remote(src, dst, ys_sem.at[s, zz], yr_sem.at[s, zz], y_peer)

    def diagonal_x(s, zz):
        src, dst = block(s, zz, True, x)
        return remote(src, dst, ds_sem.at[s, zz], dr_sem.at[s, zz], x_peer)

    def diagonal_y(s, zz, own=False):
        src, dst = block(s, zz, False, 1 - x, own)
        return remote(src, dst, ds_sem.at[s, zz], dr_sem.at[s, zz], y_peer)

    def core_send(s, zz, across, p, own=False):
        src, dst = block(s, zz, across, p, own)
        remote(src, dst, cs_sem.at[s], cr_sem.at[s], core_peer).start()

    def arrived(s, zz, across, p, sem):
        _, dst = block(s, zz, across, p)
        remote(dst, dst, cs_sem.at[s], sem, core_peer).wait_recv()

    def begin_z(s):
        for way in (0, 1):
            @pl.when(z_sends(0, way))
            def _():
                z_copy(s, 0, way).start()

    def begin_side(s):
        y_copy(s, z, own=True).start()

        @pl.when(core == 1)
        def _():
            diagonal_y(s, z, own=True).start()

        core_send(s, z, False, x, own=True)
        core_send(s, z, False, 1 - x, own=True)
        pltpu.make_async_copy(branches.at[s], gathered.at[s, me], own_sem.at[s]).start()

    def z_step(s, t):
        for way in (0, 1):
            @pl.when(z_holds(t, way))
            def _():
                arrived(s, z_of(t, way), False, x, zr_sem.at[s, t - 1, way])

                if t < nz - 1:
                    @pl.when(z_sends(t, way))
                    def _():
                        z_copy(s, t, way).start()

    def side_send(s, t):
        for way in (0, 1):
            @pl.when(z_holds(t, way))
            def _():
                zz = z_of(t, way)
                x_copy(s, zz).start()
                y_copy(s, zz).start()
                core_send(s, zz, False, x)

    def side_step(s, t):
        for way in (0,) if t == 0 else (0, 1):
            @pl.when(z_holds(t, way))
            def _():
                zz = z_of(t, way)
                arrived(s, zz, True, x, yr_sem.at[s, zz])

                @pl.when(core == 0)
                def _():
                    diagonal_x(s, zz).start()

                core_send(s, zz, True, x)
                if t > 0:
                    arrived(s, zz, False, 1 - x, xr_sem.at[s, zz])

                    @pl.when(core == 1)
                    def _():
                        diagonal_y(s, zz).start()

                    core_send(s, zz, False, 1 - x)

    def diagonal_step(s, t):
        for way in (0,) if t == 0 else (0, 1):
            @pl.when(z_holds(t, way))
            def _():
                zz = z_of(t, way)
                arrived(s, zz, True, 1 - x, dr_sem.at[s, zz])
                core_send(s, zz, True, 1 - x)

    def finish(s):
        half = gathered.at[s, pl.ds(0, n // CORES)]
        remote(half, half, cs_sem.at[s], cr_sem.at[s], core_peer).wait_recv()
        pltpu.make_async_copy(branches.at[s], gathered.at[s, me], own_sem.at[s]).wait()

    def build_onehot(s):
        @pl.loop(0, total // LANES)
        def _(i):
            rows = pl.ds(pl.multiple_of(i * LANES, LANES), LANES)
            target = lax.broadcasted_iota(jnp.int32, (LANES, total), 0) + i * LANES
            onehot[rows, :] = jnp.where(order[s : s + 1, :] == target, 1.0, 0.0).astype(BF16)

    def pick_stem():
        @pl.loop(0, total // TILE)
        def _(j):
            cols = pl.ds(pl.multiple_of(j * TILE, TILE), TILE)
            for p in range(2):
                picked[p, :, cols] = jnp.dot(
                    stem[p], onehot[:, cols], preferred_element_type=F32
                ).astype(BF16)

    def prepare(s):
        build_onehot(s)
        groups = TILE // depth

        @pl.loop(0, columns // TILE)
        def _(j):
            cols = pl.ds(pl.multiple_of(j * TILE, TILE), TILE)
            real_rows = gathered[s, :, 0, :, cols].reshape(total, TILE)
            imag_rows = gathered[s, :, 1, :, cols].reshape(total, TILE)
            for i in range(total // TILE):
                rows = onehot[i * TILE : (i + 1) * TILE, :]
                real = jnp.dot(rows, real_rows, preferred_element_type=F32)
                imag = jnp.dot(rows, imag_rows, preferred_element_type=F32)
                real_b = real.astype(BF16)
                imag_b = imag.astype(BF16)
                minus_b = (-imag).astype(BF16)
                for b in range(groups):
                    part = slice(b * depth, (b + 1) * depth)
                    at = (i * groups + b) * 2 * depth
                    wide[s - 1, 0, at : at + depth, cols] = real_b[part]
                    wide[s - 1, 0, at + depth : at + 2 * depth, cols] = minus_b[part]
                    wide[s - 1, 1, at : at + depth, cols] = imag_b[part]
                    wide[s - 1, 1, at + depth : at + 2 * depth, cols] = real_b[part]

    low_half = lax.broadcasted_iota(jnp.int32, (chunk, LANES), 1) < LANES // 2

    def pack(step, k, j, real, imag):
        for t in range(TILE // LANES):
            re = real[:, t * LANES : (t + 1) * LANES]
            im = imag[:, t * LANES : (t + 1) * LANES]
            first = jnp.where(low_half, re, pltpu.roll(im, LANES // 2, 1))
            second = jnp.where(low_half, pltpu.roll(re, LANES // 2, 1), im)
            base = (j * (TILE // LANES) + t) * 2
            send[step, k, base] = first.astype(BF16)
            send[step, k, base + 1] = second.astype(BF16)

    def swap_start(step, k):
        recv[step, k, me] = send[step, k, me]

        @pl.loop(1, n)
        def _(hop):
            target = lax.rem(me + hop, n)
            remote(
                send.at[step, k, target], recv.at[step, k, me], as_sem.at[step, k], ar_sem.at[step, k],
                {"inner": target},
            ).start()

    def swap_wait(step, k):
        part = pl.ds(0, n - 1)
        return remote(
            send.at[step, k, part], recv.at[step, k, part], as_sem.at[step, k], ar_sem.at[step, k], core_peer
        )

    def first_section(k):
        rows = slice(k * chunk, (k + 1) * chunk)

        @pl.loop(0, columns // TILE)
        def _(j):
            cols = pl.ds(pl.multiple_of(j * TILE, TILE), TILE)
            real_rows = gathered[0, :, 0, :, cols].reshape(total, TILE)
            imag_rows = gathered[0, :, 1, :, cols].reshape(total, TILE)
            a, b = picked[0, rows, :], picked[1, rows, :]
            dot = functools.partial(jnp.dot, preferred_element_type=F32)
            pack(0, k, j, dot(a, real_rows) - dot(b, imag_rows), dot(a, imag_rows) + dot(b, real_rows))

    def later_section(s, k):
        rows = slice(k * chunk, (k + 1) * chunk)

        @pl.loop(0, columns // TILE)
        def _(j):
            cols = pl.ds(pl.multiple_of(j * TILE, TILE), TILE)
            left = jnp.concatenate([recv[s - 1, k, g] for g in range(n)], axis=1)
            real = jnp.dot(left, wide[s - 1, 0, :, cols], preferred_element_type=F32)
            imag = jnp.dot(left, wide[s - 1, 1, :, cols], preferred_element_type=F32)
            if s < sections - 1:
                pack(s, k, j, real, imag)
            else:
                out[0, rows, cols] = real.astype(BF16)
                out[1, rows, cols] = imag.astype(BF16)

    def out_copy(k):
        rows = slice(k * chunk, (k + 1) * chunk)
        return pltpu.make_async_copy(out.at[:, rows], out_hbm.at[:, rows], out_sem.at[k])

    begin_z(0)
    begin_side(0)
    build_onehot(0)
    stem_copy.wait()
    pick_stem()
    for t in range(1, nz):
        z_step(0, t)
        side_send(0, t)
        if t == 1:
            begin_z(1)
        else:
            z_step(1, t - 1)
        if t == nz - 1:
            begin_z(2)
        side_step(0, t - 1)
        if t >= 2:
            diagonal_step(0, t - 2)
    side_step(0, nz - 1)
    z_step(1, nz - 1)
    diagonal_step(0, nz - 2)
    z_step(2, 1)
    diagonal_step(0, nz - 1)
    begin_side(1)
    for t in range(1, nz):
        side_send(1, t)
    finish(0)
    for k in range(CHUNKS):
        first_section(k)
        swap_start(0, k)
        if k == 0:
            for t in range(2, nz):
                z_step(2, t)
    for t in range(nz):
        side_step(1, t)
    for t in range(nz):
        diagonal_step(1, t)
    begin_side(2)
    for t in range(1, nz):
        side_send(2, t)
    finish(1)
    prepare(1)
    for k in range(CHUNKS):
        swap_wait(0, k).wait_recv()
        later_section(1, k)
        swap_start(1, k)
        if k == CHUNKS - 2:
            for t in range(nz):
                side_step(2, t)
            for t in range(nz):
                diagonal_step(2, t)
    finish(2)
    prepare(2)
    for k in range(CHUNKS):
        swap_wait(1, k).wait_recv()
        later_section(2, k)
        out_copy(k).start()

    for step in range(sections - 1):
        for k in range(CHUNKS):
            swap_wait(step, k).wait_send()
    for s in range(sections):
        for t in range(nz - 1):
            for way in (0, 1):
                @pl.when(z_sends(t, way))
                def _():
                    z_copy(s, t, way).wait_send()
        for zz in range(nz):
            @pl.when(z != zz)
            def _():
                x_copy(s, zz).wait_send()

            y_copy(s, zz).wait_send()
            diagonal_y(s, zz).wait_send()
        half = gathered.at[s, pl.ds(0, n // CORES)]
        remote(half, half, cs_sem.at[s], cr_sem.at[s], core_peer).wait_send()
    for k in range(CHUNKS):
        out_copy(k).wait()


def fused(n, stem_slab, branches, column_order):
    sections, _, depth, columns = branches.shape
    rows = stem_slab.shape[1]
    chunk = rows // CHUNKS
    nz = n // (CORES * YS)
    total = n * depth
    dma = pltpu.SemaphoreType.DMA
    return pl.pallas_call(
        functools.partial(kernel, n),
        out_shape=jax.ShapeDtypeStruct(stem_slab.shape, BF16),
        in_specs=[pl.BlockSpec(memory_space=pl.ANY)] + [pl.BlockSpec(memory_space=pltpu.VMEM)] * 2,
        out_specs=pl.BlockSpec(memory_space=pl.ANY),
        scratch_shapes=[
            pltpu.VMEM(stem_slab.shape, BF16),
            pltpu.VMEM(stem_slab.shape, BF16),
            pltpu.VMEM((sections, n, 2, depth, columns), BF16),
            pltpu.VMEM((total, total), BF16),
            pltpu.VMEM(stem_slab.shape, BF16),
            pltpu.VMEM((sections - 1, 2, 2 * total, columns), BF16),
            pltpu.VMEM((sections - 1, CHUNKS, n, chunk, LANES), BF16),
            pltpu.VMEM((sections - 1, CHUNKS, n, chunk, LANES), BF16),
            dma((sections,)),
            dma((sections, nz, 2)),
            dma((sections, nz, 2)),
            *[dma((sections, nz))] * 6,
            dma((sections,)),
            dma((sections,)),
            dma((sections - 1, CHUNKS)),
            dma((sections - 1, CHUNKS)),
            dma,
            dma((CHUNKS,)),
        ],
        compiler_params=pltpu.CompilerParams(
            collective_id=0, has_side_effects=True, vmem_limit_bytes=60 * 2**20
        ),
    )(stem_slab, branches, column_order)


def solution(mesh):
    n = mesh.shape["inner"]

    def local(stem_slab, branches, column_order):
        columns = branches.shape[3]
        fits = mesh.shape["parts"] == 2 and 2 * (columns // n) == LANES and n % (CORES * YS) == 0 and n > CORES * YS
        if fits and branches.shape[0] == 3 and columns == n * branches.shape[2]:
            return fused(n, stem_slab, branches, column_order)
        return plain(stem_slab, branches, column_order)

    in_specs = (P(None, ("parts", "inner"), None), P(None, None, "inner", None), P())
    out_specs = P(None, ("parts", "inner"), None)
    return jax.shard_map(local, mesh=mesh, in_specs=in_specs, out_specs=out_specs, check_vma=False)
```

profile of v0, /device:TPU:11, one launch (start us, length us, event | category | flops | bytes accessed | tf_op | source)
XLA Modules:
  0.0 127.7 jit_solution(12142860659103410527)
XLA Ops:
  0.0 124.7 %shard_map.37 = bf16[2,512,1024]{2,1,0:T(8,128)(2,1)} custom-call(bf16[2,512,1024]{2,1,0:T(8,128)(2,1)} %stem_hbm.1, bf16[3,2,64,1024]{3,2,1,0:T(8,128)(2,1)} %branches.1, s32[3,1024]{1,0:T(4,128)} %order.1), custom_call_target="tpu_custom_call" | custom-call | tf_op jit(solution)/shard_map/pallas_call | solution.py:386
  124.7 3.1 %copy.5 = bf16[2,512,1024]{2,1,0:T(8,128)(2,1)} copy(bf16[2,512,1024]{2,1,0:T(8,128)(2,1)} %shard_map.37) | data formatting | bytes 4194304
where the time goes:
time: 130 us; the launch traced here: 128 us
  Pallas kernels  125 us (96%)
  local copies, waits for them, and re-layouts  3.08 us (2%)
    pallas_call x1, Pallas kernels, fused(): pl.pallas_call(functools.partial(kernel, n), out_shape=jax.ShapeDtypeStru...  125 us
    unnamed x1, local copies, waits for them, and re-layouts  3.08 us

commit v1 on v0

v1 whole, which is shorter than its diff:
```python
import functools

import jax
import jax.numpy as jnp
from jax import lax
from jax.experimental import pallas as pl
from jax.experimental.pallas import tpu as pltpu
from jax.sharding import PartitionSpec as P

CORES = 2
YS = 2
CHUNKS = 2
PACK = 16
TILE = 256
LANES = 128
F32 = jnp.float32
BF16 = jnp.bfloat16
MESH_ID = pl.DeviceIdType.MESH


def add_block(ordered, block_rows):
    real_part = jnp.dot(ordered[0], block_rows[0], preferred_element_type=F32) - jnp.dot(
        ordered[1], block_rows[1], preferred_element_type=F32
    )
    imag_part = jnp.dot(ordered[0], block_rows[1], preferred_element_type=F32) + jnp.dot(
        ordered[1], block_rows[0], preferred_element_type=F32
    )
    return jnp.stack([real_part, imag_part])


def folded(slab, order_row, branch_slice):
    ordered = jnp.take(slab, order_row, axis=2)
    summed = add_block(ordered, lax.all_gather(branch_slice, "inner", axis=1, tiled=True))
    return summed.astype(BF16)


def plain(stem_slab, branches, column_order):
    current = folded(stem_slab, column_order[0], branches[0])
    for section_index in range(1, branches.shape[0]):
        current = lax.all_to_all(current, "inner", split_axis=2, concat_axis=2, tiled=True)
        current = folded(current, column_order[section_index], branches[section_index])
    return current


def kernel(
    n, stem_hbm, branches, order, out_hbm, gathered, onehot, weights, arrived, middle, turned, swapped, result, final,
    own_sem, zs_sem, zr_sem, xs_sem, xr_sem, ys_sem, yr_sem, ds_sem, dr_sem, cs_sem, cr_sem, as_sem, ar_sem,
    here_sem, out_sem,
):
    sections = branches.shape[0]
    depth = branches.shape[2]
    total = n * depth
    columns = branches.shape[3]
    part = arrived.shape[3]
    rows = n * part
    plane = CORES * YS
    nz = n // plane
    me = lax.axis_index("inner")
    x = lax.axis_index("parts")
    z = me // plane
    low = me % plane
    y = low // CORES
    core = low % CORES
    other_low = (1 - y) * CORES + core
    x_peer = {"parts": 1 - x}
    y_peer = {"inner": z * plane + other_low}
    core_peer = {"inner": z * plane + y * CORES + (1 - core)}

    barrier = pltpu.get_barrier_semaphore()

    @pl.loop(1, n)
    def _(hop):
        pl.semaphore_signal(
            barrier, inc=1, device_id={"inner": lax.rem(me + hop, n)}, device_id_type=MESH_ID
        )

    pl.semaphore_signal(barrier, inc=1, device_id=x_peer, device_id_type=MESH_ID)
    pl.semaphore_wait(barrier, n)

    def remote(src, dst, send_sem, recv_sem, device):
        return pltpu.make_async_remote_copy(
            src_ref=src, dst_ref=dst, send_sem=send_sem, recv_sem=recv_sem,
            device_id=device, device_id_type=MESH_ID,
        )


    def block(s, zz, across, p, own=False):
        slot = zz * plane + (other_low if across else low)
        return (branches.at[s, p] if own else gathered.at[s, slot, p]), gathered.at[s, slot, p]

    def z_of(t, way):
        return z - t if way == 0 else z + t

    def z_copy(s, t, way):
        src, dst = block(s, z_of(t, way), False, x, own=t == 0)
        target = {"inner": me + plane if way == 0 else me - plane}
        return remote(src, dst, zs_sem.at[s, t, way], zr_sem.at[s, t, way], target)

    def z_sends(t, way):
        return (z - t >= 0) & (z + 1 < nz) if way == 0 else (z + t < nz) & (z >= 1)

    def z_holds(t, way):
        return z - t >= 0 if way == 0 else z + t < nz

    def x_copy(s, zz):
        src, dst = block(s, zz, False, x)
        return remote(src, dst, xs_sem.at[s, zz], xr_sem.at[s, zz], x_peer)

    def y_copy(s, zz, own=False):
        src, dst = block(s, zz, False, x, own)
        return remote(src, dst, ys_sem.at[s, zz], yr_sem.at[s, zz], y_peer)

    def diagonal_x(s, zz):
        src, dst = block(s, zz, True, x)
        return remote(src, dst, ds_sem.at[s, zz], dr_sem.at[s, zz], x_peer)

    def diagonal_y(s, zz, own=False):
        src, dst = block(s, zz, False, 1 - x, own)
        return remote(src, dst, ds_sem.at[s, zz], dr_sem.at[s, zz], y_peer)

    def core_send(s, zz, across, p, own=False):
        src, dst = block(s, zz, across, p, own)
        remote(src, dst, cs_sem.at[s], cr_sem.at[s], core_peer).start()

    def landed(s, zz, across, p, sem):
        _, dst = block(s, zz, across, p)
        remote(dst, dst, cs_sem.at[s], sem, core_peer).wait_recv()

    def begin_z(s):
        for way in (0, 1):
            @pl.when(z_sends(0, way))
            def _():
                z_copy(s, 0, way).start()

    def begin_side(s):
        y_copy(s, z, own=True).start()

        @pl.when(core == 1)
        def _():
            diagonal_y(s, z, own=True).start()

        core_send(s, z, False, x, own=True)
        core_send(s, z, False, 1 - x, own=True)
        pltpu.make_async_copy(branches.at[s], gathered.at[s, me], own_sem.at[s]).start()

    def z_step(s, t):
        for way in (0, 1):
            @pl.when(z_holds(t, way))
            def _():
                landed(s, z_of(t, way), False, x, zr_sem.at[s, t - 1, way])

                if t < nz - 1:
                    @pl.when(z_sends(t, way))
                    def _():
                        z_copy(s, t, way).start()

    def side_send(s, t):
        for way in (0, 1):
            @pl.when(z_holds(t, way))
            def _():
                zz = z_of(t, way)
                x_copy(s, zz).start()
                y_copy(s, zz).start()
                core_send(s, zz, False, x)

    def side_step(s, t):
        for way in (0,) if t == 0 else (0, 1):
            @pl.when(z_holds(t, way))
            def _():
                zz = z_of(t, way)
                landed(s, zz, True, x, yr_sem.at[s, zz])
                if t > 0:
                    diagonal_x(s, zz).start()
                else:
                    @pl.when(core == 0)
                    def _():
                        diagonal_x(s, zz).start()

                core_send(s, zz, True, x)
                if t > 0:
                    landed(s, zz, False, 1 - x, xr_sem.at[s, zz])
                    core_send(s, zz, False, 1 - x)

    def diagonal_step(s, t):
        for way in (0,) if t == 0 else (0, 1):
            @pl.when(z_holds(t, way))
            def _():
                zz = z_of(t, way)
                landed(s, zz, True, 1 - x, dr_sem.at[s, zz])
                core_send(s, zz, True, 1 - x)

    def finish(s):
        half = gathered.at[s, pl.ds(0, n // CORES)]
        remote(half, half, cs_sem.at[s], cr_sem.at[s], core_peer).wait_recv()
        pltpu.make_async_copy(branches.at[s], gathered.at[s, me], own_sem.at[s]).wait()


    half_n = n // 2
    own_base = (z // (nz // 2)) * half_n
    both = pl.ds(1, 2)

    def stem_at(c, t):
        return stem_hbm.at[:, t, pl.ds(c * part, part)]

    def out_at(t, c):
        return out_hbm.at[:, t, pl.ds(c * part, part)]

    def row_source(e, t):
        return stem_at(e, t) if e < CHUNKS else turned.at[0, both, t] if e == CHUNKS else result.at[:, t]

    def row_target(e, t):
        return arrived.at[e, both, t] if e < CHUNKS else swapped.at[both, t] if e == CHUNKS else out_at(t, 1)

    def row_send(e, t):
        remote(row_source(e, t), row_target(e, me), as_sem.at[e], ar_sem.at[e], {"inner": t}).start()

    def send_far(e):
        for h in range(nz // 2):
            there = jnp.where(z < nz // 2, nz // 2 + h, nz // 2 - 1 - h) * plane

            @pl.loop(0, plane)
            def _(i):
                row_send(e, there + lax.rem(me + i, plane))

    def send_near(e):
        @pl.loop(1, half_n)
        def _(i):
            row_send(e, own_base + lax.rem(me + i, half_n))

    def rows_of(e):
        if e < CHUNKS:
            return arrived.at[e, both, pl.ds(0, n - 1)]
        if e == CHUNKS:
            return swapped.at[both, pl.ds(0, n - 1)]
        return out_hbm.at[:, pl.ds(0, n - 1), pl.ds(part, part)]

    def row_wait(e):
        part_rows = rows_of(e)
        return remote(part_rows, part_rows, as_sem.at[e], ar_sem.at[e], core_peer)

    def stem_here(c):
        return pltpu.make_async_copy(stem_at(c, me), arrived.at[c, both, me], here_sem.at[c])

    def build_onehot(s):
        @pl.loop(0, total // LANES)
        def _(i):
            span = pl.ds(pl.multiple_of(i * LANES, LANES), LANES)
            target = lax.broadcasted_iota(jnp.int32, (LANES, total), 0) + i * LANES
            onehot[span, :] = jnp.where(order[s : s + 1, :] == target, 1.0, 0.0).astype(BF16)

    def prepare(s, first=0, last=None):
        @pl.loop(first, columns // TILE if last is None else last)
        def _(j):
            cols = pl.ds(pl.multiple_of(j * TILE, TILE), TILE)
            for p in range(2):
                block_rows = gathered[s, :, p, :, cols].reshape(total, TILE)
                for i in range(total // TILE):
                    span = slice(i * TILE, (i + 1) * TILE)
                    weights[s, p, span, cols] = jnp.dot(
                        onehot[span, :], block_rows, preferred_element_type=F32
                    ).astype(BF16)

    def negate(left):
        @pl.loop(0, n)
        def _(g):
            left[0, g] = -left[2, g]

    def multiply(s, left, store):
        @pl.loop(0, columns // TILE)
        def _(j):
            cols = pl.ds(pl.multiple_of(j * TILE, TILE), TILE)
            straight = left[1:3].reshape(2 * rows, total)
            crossed = left[0:2].reshape(2 * rows, total)
            product = jnp.dot(straight, weights[s, 0, :, cols], preferred_element_type=F32) + jnp.dot(
                crossed, weights[s, 1, :, cols], preferred_element_type=F32
            )
            store(j, cols, product[:rows], product[rows:])

    low_half = lax.broadcasted_iota(jnp.int32, (part, LANES), 1) < LANES // 2

    def turn(into):
        def store(j, cols, real, imag):
            for p, value in ((1, real), (2, imag)):
                for t in range(TILE // LANES):
                    d = (j * (TILE // LANES) + t) * 2
                    lanes = slice(t * LANES, (t + 1) * LANES)
                    for h in range(n // 2):
                        first = value[2 * h * part : (2 * h + 1) * part, lanes]
                        second = value[(2 * h + 1) * part : (2 * h + 2) * part, lanes]
                        mixed = pltpu.roll(jnp.where(low_half, second, first), LANES // 2, 1)
                        at = slice(h * LANES, (h + 1) * LANES)
                        for b, block_value in ((d, jnp.where(low_half, first, mixed)), (d + 1, jnp.where(low_half, mixed, second))):
                            into[p, b, :, at] = block_value.astype(BF16)
                            if p == 2:
                                into[0, b, :, at] = (-block_value).astype(BF16)
        return store

    def keep(into):
        def store(j, cols, real, imag):
            into[0, :, :, cols] = real.astype(BF16).reshape(n, part, TILE)
            into[1, :, :, cols] = imag.astype(BF16).reshape(n, part, TILE)
        return store

    tiles = columns // TILE
    begin_z(0)
    begin_z(1)
    begin_side(0)
    begin_side(1)
    for c in range(CHUNKS):
        stem_here(c).start()
    build_onehot(0)
    z_step(0, 1)
    side_send(0, 1)
    begin_z(2)
    z_step(1, 1)
    side_send(1, 1)
    side_step(0, 0)
    z_step(0, 2)
    side_send(0, 2)
    z_step(2, 1)
    send_far(0)
    z_step(1, 2)
    side_send(1, 2)
    side_step(0, 1)
    z_step(0, 3)
    side_send(0, 3)
    side_step(1, 0)
    side_step(0, 2)
    diagonal_step(0, 0)
    z_step(1, 3)
    side_send(1, 3)
    side_step(1, 1)
    send_near(0)
    z_step(2, 2)
    side_step(0, 3)
    diagonal_step(0, 1)
    side_step(1, 2)
    send_far(1)
    diagonal_step(0, 2)
    side_step(1, 3)
    diagonal_step(0, 3)
    send_near(1)
    finish(0)
    prepare(0, 0, tiles // 2)
    diagonal_step(1, 0)
    z_step(2, 3)
    diagonal_step(1, 1)
    prepare(0, tiles // 2, tiles)
    diagonal_step(1, 2)
    diagonal_step(1, 3)
    begin_side(2)
    for t in range(1, nz):
        side_send(2, t)
    build_onehot(1)
    stem_here(0).wait()
    row_wait(0).wait_recv()
    negate(arrived.at[0])
    multiply(0, arrived.at[0], turn(middle))
    finish(1)
    prepare(1)
    multiply(1, middle, turn(turned.at[0]))
    swapped[both, me] = turned[0, both, me]
    send_far(2)
    send_near(2)
    build_onehot(2)
    side_step(2, 0)
    side_step(2, 1)
    stem_here(1).wait()
    row_wait(1).wait_recv()
    negate(arrived.at[1])
    multiply(0, arrived.at[1], turn(middle))
    for t in range(2, nz):
        side_step(2, t)
    multiply(1, middle, turn(turned.at[1]))
    for t in range(nz):
        diagonal_step(2, t)
    finish(2)
    prepare(2)
    multiply(2, turned.at[1], keep(result))
    send_far(3)
    send_near(3)
    own_out = pltpu.make_async_copy(result.at[:, me], out_at(me, 1), here_sem.at[0])
    own_out.start()
    row_wait(2).wait_recv()
    negate(swapped)
    multiply(2, swapped, keep(final))
    first_out = pltpu.make_async_copy(final, out_hbm.at[:, :, pl.ds(0, part)], out_sem)
    first_out.start()

    for s in range(sections):
        for t in range(nz - 1):
            for way in (0, 1):
                @pl.when(z_sends(t, way))
                def _():
                    z_copy(s, t, way).wait_send()
        for zz in range(nz):
            @pl.when(z != zz)
            def _():
                x_copy(s, zz).wait_send()

            y_copy(s, zz).wait_send()
            diagonal_y(s, zz).wait_send()
        half = gathered.at[s, pl.ds(0, n // CORES)]
        remote(half, half, cs_sem.at[s], cr_sem.at[s], core_peer).wait_send()
    for e in range(2 * CHUNKS):
        row_wait(e).wait_send()
    own_out.wait()
    first_out.wait()
    row_wait(3).wait_recv()


def fused(n, stem_slab, branches, column_order):
    sections, _, depth, columns = branches.shape
    share = stem_slab.shape[1] // n
    part = share // CHUNKS
    nz = n // (CORES * YS)
    total = n * depth
    dma = pltpu.SemaphoreType.DMA
    stem = stem_slab.reshape(2, n, share, columns)
    result = pl.pallas_call(
        functools.partial(kernel, n),
        out_shape=jax.ShapeDtypeStruct(stem.shape, BF16),
        in_specs=[pl.BlockSpec(memory_space=pl.ANY)] + [pl.BlockSpec(memory_space=pltpu.VMEM)] * 2,
        out_specs=pl.BlockSpec(memory_space=pl.ANY),
        scratch_shapes=[
            pltpu.VMEM((sections, n, 2, depth, columns), BF16),
            pltpu.VMEM((total, total), BF16),
            pltpu.VMEM((sections, 2, total, columns), BF16),
            pltpu.VMEM((CHUNKS, 3, n, part, columns), BF16),
            pltpu.VMEM((3, n, part, columns), BF16),
            pltpu.VMEM((CHUNKS, 3, n, part, columns), BF16),
            pltpu.VMEM((3, n, part, columns), BF16),
            pltpu.VMEM((2, n, part, columns), BF16),
            pltpu.VMEM((2, n, part, columns), BF16),
            dma((sections,)),
            dma((sections, nz, 2)),
            dma((sections, nz, 2)),
            *[dma((sections, nz))] * 6,
            dma((sections,)),
            dma((sections,)),
            dma((2 * CHUNKS,)),
            dma((2 * CHUNKS,)),
            dma((CHUNKS,)),
            dma,
        ],
        compiler_params=pltpu.CompilerParams(
            collective_id=0, has_side_effects=True, vmem_limit_bytes=60 * 2**20
        ),
    )(stem, branches, column_order)
    return result.reshape(stem_slab.shape)


def solution(mesh):
    n = mesh.shape["inner"]

    def local(stem_slab, branches, column_order):
        columns = branches.shape[3]
        fits = mesh.shape["parts"] == 2 and 2 * (columns // n) == LANES and n == 4 * CORES * YS
        even = stem_slab.shape[1] == n * CHUNKS * PACK and columns % TILE == 0
        if fits and even and branches.shape[0] == 3 and columns == n * branches.shape[2]:
            return fused(n, stem_slab, branches, column_order)
        return plain(stem_slab, branches, column_order)

    in_specs = (P(None, ("parts", "inner"), None), P(None, None, "inner", None), P())
    out_specs = P(None, ("parts", "inner"), None)
    return jax.shard_map(local, mesh=mesh, in_specs=in_specs, out_specs=out_specs, check_vma=False)
```

time: 130 us -> 123 us (0.946)
  the two profiles are of different devices: /device:TPU:11 before, /device:TPU:1 now
where the time goes in v1:
time: 123 us
  Pallas kernels  120 us (98%)
  local copies, waits for them, and re-layouts  3.08 us (3%)
    pallas_call x1, Pallas kernels, fused(): pl.pallas_call(functools.partial(kernel, n), out_shape=jax.ShapeDtypeStru...  120 us
    unnamed x1, local copies, waits for them, and re-layouts  3.08 us

profile of v1, /device:TPU:1, one launch (start us, length us, event | category | flops | bytes accessed | tf_op | source)
XLA Modules:
  0.0 122.8 jit_solution(4728080118347238372)
XLA Ops:
  0.0 119.7 %shard_map.37 = bf16[2,16,32,1024]{3,2,1,0:T(8,128)(2,1)} custom-call(bf16[2,16,32,1024]{3,2,1,0:T(8,128)(2,1)} %bitcast.3, bf16[3,2,64,1024]{3,2,1,0:T(8,128)(2,1)} %branches.1, s32[3,1024]{1,0:T(4,128)} %order.1), custom_call_target="tpu_custom_call" | custom-call | tf_op jit(solution)/shard_map/pallas_call | solution.py:420
  119.7 3.1 %copy.5 = bf16[2,512,1024]{2,1,0:T(8,128)(2,1)} copy(bf16[2,512,1024]{2,1,0:T(8,128)(2,1)} %bitcast.2) | data formatting | bytes 4194304

commit v2 on v1

--- a/solution.py
+++ b/solution.py
@@ -43,9 +43,9 @@
 
 
 def kernel(
-    n, stem_hbm, branches, order, out_hbm, gathered, onehot, weights, arrived, middle, turned, swapped, result, final,
+    n, stem_hbm, branches_hbm, order_hbm, out_hbm, branches, order, gathered, onehot, weights, arrived, middle, turned, swapped, result, final,
     own_sem, zs_sem, zr_sem, xs_sem, xr_sem, ys_sem, yr_sem, ds_sem, dr_sem, cs_sem, cr_sem, as_sem, ar_sem,
-    here_sem, out_sem,
+    here_sem, out_sem, in_sem,
 ):
     sections = branches.shape[0]
     depth = branches.shape[2]
@@ -66,6 +66,18 @@
     y_peer = {"inner": z * plane + other_low}
     core_peer = {"inner": z * plane + y * CORES + (1 - core)}
 
+    branches_in = pltpu.make_async_copy(branches_hbm, branches, in_sem.at[0])
+    branches_in.start()
+    order_in = pltpu.make_async_copy(order_hbm, order, in_sem.at[1])
+    order_in.start()
+    stem_in = [
+        pltpu.make_async_copy(
+            stem_hbm.at[:, me, pl.ds(c * part, part)], arrived.at[c, pl.ds(1, 2), me], here_sem.at[c]
+        )
+        for c in range(CHUNKS)
+    ]
+    for copy in stem_in:
+        copy.start()
     barrier = pltpu.get_barrier_semaphore()
 
     @pl.loop(1, n)
@@ -214,8 +226,8 @@
     def row_send(e, t):
         remote(row_source(e, t), row_target(e, me), as_sem.at[e], ar_sem.at[e], {"inner": t}).start()
 
-    def send_far(e):
-        for h in range(nz // 2):
+    def send_far(e, planes):
+        for h in planes:
             there = jnp.where(z < nz // 2, nz // 2 + h, nz // 2 - 1 - h) * plane
 
             @pl.loop(0, plane)
@@ -237,9 +249,6 @@
     def row_wait(e):
         part_rows = rows_of(e)
         return remote(part_rows, part_rows, as_sem.at[e], ar_sem.at[e], core_peer)
-
-    def stem_here(c):
-        return pltpu.make_async_copy(stem_at(c, me), arrived.at[c, both, me], here_sem.at[c])
 
     def build_onehot(s):
         @pl.loop(0, total // LANES)
@@ -302,12 +311,13 @@
         return store
 
     tiles = columns // TILE
+    outward = tuple(range(nz // 2))
+    branches_in.wait()
     begin_z(0)
     begin_z(1)
     begin_side(0)
     begin_side(1)
-    for c in range(CHUNKS):
-        stem_here(c).start()
+    order_in.wait()
     build_onehot(0)
     z_step(0, 1)
     side_send(0, 1)
@@ -318,9 +328,9 @@
     z_step(0, 2)
     side_send(0, 2)
     z_step(2, 1)
-    send_far(0)
     z_step(1, 2)
     side_send(1, 2)
+    send_far(0, outward)
     side_step(0, 1)
     z_step(0, 3)
     side_send(0, 3)
@@ -335,49 +345,54 @@
     side_step(0, 3)
     diagonal_step(0, 1)
     side_step(1, 2)
-    send_far(1)
     diagonal_step(0, 2)
+    send_far(1, outward[::-1])
     side_step(1, 3)
     diagonal_step(0, 3)
     send_near(1)
+    begin_side(2)
+    side_send(2, 1)
+    side_send(2, 2)
     finish(0)
     prepare(0, 0, tiles // 2)
     diagonal_step(1, 0)
-    z_step(2, 3)
     diagonal_step(1, 1)
     prepare(0, tiles // 2, tiles)
     diagonal_step(1, 2)
     diagonal_step(1, 3)
-    begin_side(2)
-    for t in range(1, nz):
-        side_send(2, t)
     build_onehot(1)
-    stem_here(0).wait()
+    finish(1)
+    prepare(1, 0, tiles // 2)
+    side_step(2, 0)
+    z_step(2, 3)
+    side_send(2, 3)
+    prepare(1, tiles // 2, tiles)
+    stem_in[0].wait()
     row_wait(0).wait_recv()
     negate(arrived.at[0])
     multiply(0, arrived.at[0], turn(middle))
-    finish(1)
-    prepare(1)
+    diagonal_step(2, 0)
     multiply(1, middle, turn(turned.at[0]))
     swapped[both, me] = turned[0, both, me]
-    send_far(2)
+    send_far(2, outward[:1])
+    build_onehot(2)
+    side_step(2, 1)
+    stem_in[1].wait()
+    row_wait(1).wait_recv()
+    send_far(2, outward[1:])
     send_near(2)
-    build_onehot(2)
-    side_step(2, 0)
-    side_step(2, 1)
-    stem_here(1).wait()
-    row_wait(1).wait_recv()
+    side_step(2, 2)
     negate(arrived.at[1])
     multiply(0, arrived.at[1], turn(middle))
-    for t in range(2, nz):
-        side_step(2, t)
+    side_step(2, 3)
+    diagonal_step(2, 1)
     multiply(1, middle, turn(turned.at[1]))
-    for t in range(nz):
-        diagonal_step(2, t)
+    diagonal_step(2, 2)
+    diagonal_step(2, 3)
     finish(2)
     prepare(2)
     multiply(2, turned.at[1], keep(result))
-    send_far(3)
+    send_far(3, outward[::-1])
     send_near(3)
     own_out = pltpu.make_async_copy(result.at[:, me], out_at(me, 1), here_sem.at[0])
     own_out.start()
@@ -419,10 +434,12 @@
     stem = stem_slab.reshape(2, n, share, columns)
     result = pl.pallas_call(
         functools.partial(kernel, n),
-        out_shape=jax.ShapeDtypeStruct(stem.shape, BF16),
-        in_specs=[pl.BlockSpec(memory_space=pl.ANY)] + [pl.BlockSpec(memory_space=pltpu.VMEM)] * 2,
+        out_shape=pltpu.VMEM(stem.shape, BF16),
+        in_specs=[pl.BlockSpec(memory_space=pltpu.HBM)] * 3,
         out_specs=pl.BlockSpec(memory_space=pl.ANY),
         scratch_shapes=[
+            pltpu.VMEM(branches.shape, BF16),
+            pltpu.VMEM(column_order.shape, jnp.int32),
             pltpu.VMEM((sections, n, 2, depth, columns), BF16),
             pltpu.VMEM((total, total), BF16),
             pltpu.VMEM((sections, 2, total, columns), BF16),
@@ -442,9 +459,10 @@
             dma((2 * CHUNKS,)),
             dma((CHUNKS,)),
             dma,
+            dma((2,)),
         ],
         compiler_params=pltpu.CompilerParams(
-            collective_id=0, has_side_effects=True, vmem_limit_bytes=60 * 2**20
+            collective_id=0, has_side_effects=True, vmem_limit_bytes=61 * 2**20
         ),
     )(stem, branches, column_order)
     return result.reshape(stem_slab.shape)

time: 123 us -> 115 us (0.935)
  the two profiles are of different devices: /device:TPU:1 before, /device:TPU:11 now
where the time goes in v2:
time: 115 us
  Pallas kernels  113 us (98%)
  local copies, waits for them, and re-layouts  1.32 us (1%)
    pallas_call x1, Pallas kernels, fused(): pl.pallas_call(functools.partial(kernel, n), out_shape=pltpu.VMEM(stem.sh...  113 us

profile of v2, /device:TPU:11, one launch (start us, length us, event | category | flops | bytes accessed | tf_op | source)
XLA Modules:
  0.0 114.6 jit_solution(10036816773804904918)
XLA Ops:
  0.0 113.3 %shard_map.37 = bf16[2,16,32,1024]{3,2,1,0:T(8,128)(2,1)S(1)} custom-call(bf16[2,16,32,1024]{3,2,1,0:T(8,128)(2,1)} %bitcast.3, bf16[3,2,64,1024]{3,2,1,0:T(8,128)(2,1)} %branches_hbm.1, s32[3,1024]{1,0:T(4,128)} %order_hbm.1), custom_call_target="tpu_custom_call" | custom-call | tf_op jit(solution)/shard_map/pallas_call | solution.py:435
  113.3 1.3 %copy.5 = bf16[2,512,1024]{2,1,0:T(8,128)(2,1)} copy(bf16[2,512,1024]{2,1,0:T(8,128)(2,1)S(1)} %bitcast.2) | data formatting | bytes 4194304

commit v3 on v2

--- a/solution.py
+++ b/solution.py
@@ -45,7 +45,7 @@
 def kernel(
     n, stem_hbm, branches_hbm, order_hbm, out_hbm, branches, order, gathered, onehot, weights, arrived, middle, turned, swapped, result, final,
     own_sem, zs_sem, zr_sem, xs_sem, xr_sem, ys_sem, yr_sem, ds_sem, dr_sem, cs_sem, cr_sem, as_sem, ar_sem,
-    here_sem, out_sem, in_sem,
+    here_sem, out_sem, in_sem, order_sem, meet_sem,
 ):
     sections = branches.shape[0]
     depth = branches.shape[2]
@@ -66,9 +66,12 @@
     y_peer = {"inner": z * plane + other_low}
     core_peer = {"inner": z * plane + y * CORES + (1 - core)}
 
-    branches_in = pltpu.make_async_copy(branches_hbm, branches, in_sem.at[0])
-    branches_in.start()
-    order_in = pltpu.make_async_copy(order_hbm, order, in_sem.at[1])
+    branches_in = [
+        pltpu.make_async_copy(branches_hbm.at[s], branches.at[s], in_sem.at[s]) for s in range(sections)
+    ]
+    for copy in branches_in:
+        copy.start()
+    order_in = pltpu.make_async_copy(order_hbm, order, order_sem)
     order_in.start()
     stem_in = [
         pltpu.make_async_copy(
@@ -80,14 +83,29 @@
         copy.start()
     barrier = pltpu.get_barrier_semaphore()
 
-    @pl.loop(1, n)
-    def _(hop):
-        pl.semaphore_signal(
-            barrier, inc=1, device_id={"inner": lax.rem(me + hop, n)}, device_id_type=MESH_ID
-        )
+
+    def greet(sem):
+        for peer in (y_peer, core_peer):
+            pl.semaphore_signal(sem, inc=1, device_id=peer, device_id_type=MESH_ID)
+
+        @pl.when(z + 1 < nz)
+        def _():
+            pl.semaphore_signal(sem, inc=1, device_id={"inner": me + plane}, device_id_type=MESH_ID)
+
+        @pl.when(z >= 1)
+        def _():
+            pl.semaphore_signal(sem, inc=1, device_id={"inner": me - plane}, device_id_type=MESH_ID)
+
+    greeted = 2 + jnp.where(z + 1 < nz, 1, 0) + jnp.where(z >= 1, 1, 0)
+
+    def meet(i):
+        pl.semaphore_wait(meet_sem.at[i], greeted)
+        if i + 1 < nz:
+            greet(meet_sem.at[i + 1])
 
     pl.semaphore_signal(barrier, inc=1, device_id=x_peer, device_id_type=MESH_ID)
-    pl.semaphore_wait(barrier, n)
+    greet(barrier)
+    pl.semaphore_wait(barrier, greeted + 1)
 
     def remote(src, dst, send_sem, recv_sem, device):
         return pltpu.make_async_remote_copy(
@@ -312,8 +330,10 @@
 
     tiles = columns // TILE
     outward = tuple(range(nz // 2))
-    branches_in.wait()
+    branches_in[0].wait()
     begin_z(0)
+    greet(meet_sem.at[0])
+    branches_in[1].wait()
     begin_z(1)
     begin_side(0)
     begin_side(1)
@@ -321,15 +341,20 @@
     build_onehot(0)
     z_step(0, 1)
     side_send(0, 1)
+    meet(0)
+    branches_in[2].wait()
     begin_z(2)
     z_step(1, 1)
     side_send(1, 1)
+    meet(1)
     side_step(0, 0)
     z_step(0, 2)
     side_send(0, 2)
+    meet(2)
     z_step(2, 1)
     z_step(1, 2)
     side_send(1, 2)
+    meet(3)
     send_far(0, outward)
     side_step(0, 1)
     z_step(0, 3)
@@ -377,16 +402,16 @@
     send_far(2, outward[:1])
     build_onehot(2)
     side_step(2, 1)
+    side_step(2, 2)
+    side_step(2, 3)
     stem_in[1].wait()
     row_wait(1).wait_recv()
     send_far(2, outward[1:])
     send_near(2)
-    side_step(2, 2)
     negate(arrived.at[1])
     multiply(0, arrived.at[1], turn(middle))
-    side_step(2, 3)
+    multiply(1, middle, turn(turned.at[1]))
     diagonal_step(2, 1)
-    multiply(1, middle, turn(turned.at[1]))
     diagonal_step(2, 2)
     diagonal_step(2, 3)
     finish(2)
@@ -459,7 +484,9 @@
             dma((2 * CHUNKS,)),
             dma((CHUNKS,)),
             dma,
-            dma((2,)),
+            dma((sections,)),
+            dma,
+            pltpu.SemaphoreType.REGULAR((nz,)),
         ],
         compiler_params=pltpu.CompilerParams(
             collective_id=0, has_side_effects=True, vmem_limit_bytes=61 * 2**20

time: 115 us -> 114 us (level)
  no operation moved by 1% of the time
where the time goes in v3:
time: 114 us
  Pallas kernels  113 us (99%)
  local copies, waits for them, and re-layouts  1.32 us (1%)
    pallas_call x1, Pallas kernels, fused(): pl.pallas_call(functools.partial(kernel, n), out_shape=pltpu.VMEM(stem.sh...  113 us

profile of v3, /device:TPU:11, one launch (start us, length us, event | category | flops | bytes accessed | tf_op | source)
XLA Modules:
  0.0 114.2 jit_solution(4400126734992553554)
XLA Ops:
  0.0 112.9 %shard_map.37 = bf16[2,16,32,1024]{3,2,1,0:T(8,128)(2,1)S(1)} custom-call(bf16[2,16,32,1024]{3,2,1,0:T(8,128)(2,1)} %bitcast.3, bf16[3,2,64,1024]{3,2,1,0:T(8,128)(2,1)} %branches_hbm.1, s32[3,1024]{1,0:T(4,128)} %order_hbm.1), custom_call_target="tpu_custom_call" | custom-call | tf_op jit(solution)/shard_map/pallas_call | solution.py:460
  112.9 1.3 %copy.5 = bf16[2,512,1024]{2,1,0:T(8,128)(2,1)} copy(bf16[2,512,1024]{2,1,0:T(8,128)(2,1)S(1)} %bitcast.2) | data formatting | bytes 4194304
